TPU v7x, 32 devices: a whole 2x2x4 slice. The times are simulated.
32 devices in a mesh: grp: 8 (over z, x), dom: 4 (over y, core).
Axes of the slice: x: 2, y: 2, z: 4, core: 2. Of those that a mesh axis runs over, the one named last changes fastest.
Arguments:
- positions: float32 [3, 4096, 512], P(None, ('grp', 'dom')), may hold values from 0 to 1
- velocities: float32 [3, 4096, 512], P(None, ('grp', 'dom')), may hold values from -6 to 6
- masses: float32 [4096, 512], P(('grp', 'dom')), may hold values from 0.5 to 2
- block_halo: int32 [4096], P(('grp', 'dom')), may hold values from 0 to 4095, as said below
- block_shift: int32 [3, 4096], P(None, ('grp', 'dom')), may hold values from -1 to 1
- block_live: int32 [4096], P(('grp', 'dom')), may hold values from 64 to 512
- block_count: int32 [32], P(('grp', 'dom')), may hold values from 32 to 128
- home_slot: int32 [4096], replicated, may hold values from 0 to 4095, as said below
Outputs:
- halo_table: float32 [11, 4096], P(None, ('grp', 'dom'))
- kinetic: float32 [4096, 512], P(('grp', 'dom'))
- radial: float32 [4096, 512], P(('grp', 'dom'))
Inputs may be any that keep to these rules, and one draw needn't show every extreme that they name: A permutation: the halo h is owned by the device of index home_slot[h] // 128 (grp+dom order), in its column home_slot[h] % 128. `block_halo`: the owner of a block's halo lies in the block's own index of grp or in the next one (index + 1, wrapping around); both occur.
All inputs are finite; a program needn't handle non-finite values.
Results may differ from a plain program's by a relative error of at most 0.0003.
Values sent between devices are 32-bit elements; how exact they have to be, the bound alone decides.
A program may use at most 64 MiB of HBM per device.

v0:
```python
import jax
import jax.numpy as jnp
from jax import lax
from jax.sharding import PartitionSpec as P

BOX = 1.0
EPSILON = 1e-06


def from_behind(shard, axis, by):
    devices = lax.axis_size(axis)
    return lax.ppermute(shard, axis, [(i, (i + by) % devices) for i in range(devices)])


def crossed(first, second):
    return jnp.stack(
        [
            first[1] * second[2] - first[2] * second[1],
            first[2] * second[0] - first[0] * second[2],
            first[0] * second[1] - first[1] * second[0],
        ]
    )


def block_moments(positions, velocities, masses, block_shift, block_live, valid):
    lanes = jnp.arange(masses.shape[1], dtype=jnp.int32)
    live_mask = ((lanes[None, :] < block_live[:, None]) & valid[:, None]).astype(masses.dtype)
    weights = masses * live_mask
    unwrapped = positions + BOX * block_shift.astype(positions.dtype)[:, :, None]
    speed_sq = jnp.sum(velocities * velocities, axis=0)
    angular = crossed(unwrapped, velocities)
    rows = [
        jnp.sum(weights, axis=1)[None],
        jnp.sum(weights * unwrapped, axis=2),
        jnp.sum(weights * velocities, axis=2),
        jnp.sum(weights * speed_sq, axis=1)[None],
        jnp.sum(weights * angular, axis=2),
    ]
    return (jnp.concatenate(rows, axis=0), live_mask, unwrapped)


def halo_properties(sums, total, halos):
    heavy = jnp.maximum(sums[0], 1.0)
    centre = sums[1:4] / heavy
    drift = sums[4:7] / heavy
    spread = sums[7] / heavy - jnp.sum(drift * drift, axis=0)
    spin = sums[8:11] / heavy - crossed(centre, drift)
    share = sums[0] * halos / total
    return jnp.concatenate([share[None], centre, drift, spread[None], spin], axis=0)


def particle_outputs(unwrapped, velocities, live_mask, stats):
    centre = stats[0:3][:, :, None]
    drift = stats[3:6][:, :, None]
    spread = stats[6][:, None]
    offset = velocities - drift
    kinetic = jnp.sum(offset * offset, axis=0) / (3.0 * spread + EPSILON)
    distance = unwrapped - centre
    radial = jnp.sum(distance * distance, axis=0)
    return (kinetic * live_mask, radial * live_mask)


def local(
    positions, velocities, masses, block_halo, block_shift, block_live, block_count, home_slot
):
    blocks = masses.shape[0]
    halos = home_slot.shape[0]
    owned_count = halos // lax.axis_size(("grp", "dom"))
    valid = jnp.arange(blocks, dtype=jnp.int32) < block_count[0]
    moments, live_mask, unwrapped = block_moments(
        positions, velocities, masses, block_shift, block_live, valid
    )
    slots = home_slot[block_halo]
    domains = lax.axis_size("dom")
    slab_groups = lax.axis_size("grp")
    window = domains * owned_count
    owner = slots // owned_count
    relative = (owner // domains - lax.axis_index("grp")) % slab_groups
    local_column = relative * window + owner % domains * owned_count + slots % owned_count
    table = jnp.zeros((11, 2 * window), jnp.float32).at[:, local_column].add(moments)
    total = lax.psum(jnp.sum(moments[0]), ("grp", "dom"))
    arrived = from_behind(table[:, window:], "grp", 1)
    owned_sums = lax.psum_scatter(
        table[:, :window] + arrived, "dom", scatter_dimension=1, tiled=True
    )
    halo_table = halo_properties(owned_sums, total, halos)
    group_stats = lax.all_gather(halo_table[1:8], "dom", axis=1, tiled=True)
    returned = from_behind(group_stats, "grp", -1)
    stats = jnp.concatenate([group_stats, returned], axis=1)[:, local_column]
    kinetic, radial = particle_outputs(unwrapped, velocities, live_mask, stats)
    return (halo_table, kinetic, radial)


def solution(mesh):
    return jax.shard_map(
        local,
        mesh=mesh,
        in_specs=(
            P(None, ("grp", "dom"), None),
            P(None, ("grp", "dom"), None),
            P(("grp", "dom"), None),
            P(("grp", "dom")),
            P(None, ("grp", "dom")),
            P(("grp", "dom")),
            P(("grp", "dom")),
            P(),
        ),
        out_specs=(P(None, ("grp", "dom")), P(("grp", "dom"), None), P(("grp", "dom"), None)),
        check_vma=False,
    )
```

profile of v0, /device:TPU:0, one launch (start us, length us, event | category | flops | bytes accessed | tf_op | source)
XLA Modules:
  0.0 85.7 jit_solution(2616663069370021129)
XLA Ops:
  7.2 0.7 convert_element_type.4
  8.6 1.3 %broadcast_add_fusion = f32[3,128,512]{2,1,0:T(8,128)S(1)} fusion(f32[3,128,512]{2,1,0:T(8,128)} %param.8, f32[3,128]{1,0:T(4,128)S(1)} %convert_element_type.4), kind=kLoop, calls=%fused_computation.10 | loop fusion | flops 196608 | bytes 1574400 | tf_op jit(solution)/shard_map/add | solution.py:29
  10.1 0.8 copy-done.3
  11.2 0.4 multiply_reduce_fusion.2
  11.6 0.8 fusion.16
  12.5 0.5 copy-done.5
  13.1 1.1 %gather_fusion = s32[128]{0:T(128)S(1)} fusion(s32[4096]{0:T(1024)S(1)} %copy-done, s32[1024]{0:T(1024)S(1)} %pad_clamp_fusion.1), kind=kCustom, calls=%fused_computation | custom fusion | bytes 1536 | tf_op jit(solution)/shard_map/gather | solution.py:73
  14.3 1.1 %scatter_custom_fusion = f32[11,1024]{0,1:T(8,128)S(1)} fusion(s32[128]{0:T(128)S(1)} %fusion.13, f32[128,11]{1,0:T(8,128)S(1)} %copy.44, f32[]{:T(128)} %constant.66.clone.1), kind=kCustom, calls=%fused_computation.17 | custom fusion | flops 1408 | bytes 45060 | tf_op jit(solution)/shard_map/scatter-add | solution.py:80
  15.6 3.0 %collective-permute-start = (f32[11,512]{1,0:T(8,128)S(1)}, f32[11,512]{1,0:T(8,128)S(1)}, u32[]{:S(2)}, u32[]{:S(2)}) collective-permute-start(f32[11,512]{1,0:T(8,128)S(1)} %copy.51), channel_id=1, source_target_pairs={{0,4},{4,8},{8,12},{12,16},{16,20},{20,24},{24,28},{28,0},{1,5},{5... | collective-permute-start | bytes 67592 | tf_op jit(solution)/shard_map/ppermute | solution.py:12
  18.7 4.8 %collective-permute-done = f32[11,512]{1,0:T(8,128)S(1)} collective-permute-done((f32[11,512]{1,0:T(8,128)S(1)}, f32[11,512]{1,0:T(8,128)S(1)}, u32[]{:S(2)}, u32[]{:S(2)}) %collective-permute-start) | collective-permute-done | bytes 22560 | tf_op jit(solution)/shard_map/ppermute | solution.py:12
  23.5 0.6 add.129
  24.2 38.2 %psum.7 = f32[]{:T(128)} all-reduce(f32[]{:T(128)} %get-tuple-element.13), channel_id=1, replica_groups=mesh['grp'=8,'dom'=4] {'grp','dom'}, use_global_device_ids=true, to_apply=%region_9.10 | all-reduce | flops 1 | bytes 8 | tf_op jit(solution)/shard_map/psum | solution.py:81
  62.4 0.7 fusion.15
  63.1 0.8 multiply_reduce_fusion.6
  63.9 1.4 %fusion.14 = (f32[1,128]{1,0:T(1,128)S(1)}, f32[1,128]{1,0:T(1,128)S(1)}) fusion(f32[11,128]{1,0:T(8,128)} %reduce-scatter.2.cloned.1.call-done, f32[128]{0:T(128)S(1)} %get-tuple-element.16, f32[]{:T(128)} %psum.7), kind=kLoop, calls=%fused_computation.55 | loop fusion | flops 640 | bytes 2564 | tf_op jit(solution)/shard_map/sub | solution.py:46
  65.3 5.7 %all_gather.3 = f32[7,512]{1,0:T(8,128)S(1)} all-gather(f32[7,128]{1,0:T(8,128)S(1)} %pad_maximum_fusion.1), channel_id=1, replica_groups=mesh['grp'=8,'dom'=4] {'dom'}, dimensions={1}, use_global_device_ids=true | all-gather | bytes 17920 | tf_op jit(solution)/shard_map/all_gather | solution.py:87
  71.1 3.4 %collective-permute-start.1 = (f32[7,512]{1,0:T(8,128)S(1)}, f32[7,512]{1,0:T(8,128)S(1)}, u32[]{:S(2)}, u32[]{:S(2)}) collective-permute-start(f32[7,512]{1,0:T(8,128)S(1)} %all_gather.3), channel_id=1, source_target_pairs={{0,28},{4,0},{8,4},{12,8},{16,12},{20,16},{24,20},{28,24},{1,29},{... | collective-permute-start | bytes 43016 | tf_op jit(solution)/shard_map/ppermute | solution.py:12
  74.4 0.7 divide_subtract_fusion
  75.1 1.2 %concatenate.13 = f32[11,128]{1,0:T(8,128)} concatenate(f32[1,128]{1,0:T(1,128)S(1)} %get-tuple-element.27, f32[3,128]{1,0:T(4,128)S(1)} %get-tuple-element.25, f32[3,128]{1,0:T(4,128)S(1)} %get-tuple-element.17, f32[1,128]{1,0:T(1,128)S(1)} %get-tuple-element.26, f32[3,128]{1,0:T(4,128)S(1)} %divide_subtract_fusion), dimensions={0} | concatenate | bytes 11264 | tf_op jit(solution)/shard_map/concatenate | solution.py:49
  76.3 0.2 copy.47
  76.6 0.7 gather_fusion.1
  77.3 0.2 fusion.7
  77.6 0.3 multiply_reduce_fusion
  77.9 0.9 %fusion.4 = (f32[128,512]{1,0:T(8,128)}, f32[128,512]{1,0:T(8,128)}) fusion(f32[128,512]{1,0:T(8,128)S(1)} %get-tuple-element.33, s32[128]{0:T(128)S(1)} %copy-done.4, pred[128]{0:T(512)(128)(4,1)S(1)} %iota_compare_fusion.1, f32[128,512]{1,0:T(8,128)S(1)} %get-tuple-element.34, f32[128]{0:T(128)S(1)} %fusion.7), kind=kLoop, calls=%fused_computation.20 | loop fusion | flops 327680 | bytes 1049728 | tf_op jit(solution)/shard_map/mul | solution.py:60
  (32 shorter events, 1.3 us)
Async XLA Ops:
  7.2 5.9 %copy-start = (s32[4096]{0:T(1024)S(1)}, s32[4096]{0:T(1024)}, u32[]{:S(2)}) copy-start(s32[4096]{0:T(1024)} %param.15) | copy-start | bytes 49156
  7.2 55.2 %reduce-scatter.2.cloned.1.call-start = ((), (), s32[]{:S(2)}) async-start(), calls=%async_computation.1 | async-start | bytes 40960 | tf_op jit(solution)/shard_map/reduce_scatter | solution.py:83
  8.6 1.4 %copy-start.2 = (f32[3,128,512]{2,1,0:T(8,128)S(1)}, f32[3,128,512]{2,1,0:T(8,128)}, u32[]{:S(2)}) copy-start(f32[3,128,512]{2,1,0:T(8,128)} %param.9) | copy-start | bytes 2359300
  10.0 0.9 %copy-start.3 = (f32[128,512]{1,0:T(8,128)S(1)}, f32[128,512]{1,0:T(8,128)}, u32[]{:S(2)}) copy-start(f32[128,512]{1,0:T(8,128)} %param.10) | copy-start | bytes 786436
  10.0 1.0 %copy-start.4 = (s32[128]{0:T(128)S(1)}, s32[128]{0:T(128)}, u32[]{:S(2)}) copy-start(s32[128]{0:T(128)} %param.13) | copy-start | bytes 1540
  10.0 1.2 %copy-start.1 = (f32[3,128,512]{2,1,0:T(8,128)S(1)}, f32[3,128,512]{2,1,0:T(8,128)}, u32[]{:S(2)}) copy-start(f32[3,128,512]{2,1,0:T(8,128)} %param.8) | copy-start | bytes 2359300
  12.4 0.7 copy-start.5
  15.6 7.9 %collective-permute-start = (f32[11,512]{1,0:T(8,128)S(1)}, f32[11,512]{1,0:T(8,128)S(1)}, u32[]{:S(2)}, u32[]{:S(2)}) collective-permute-start(f32[11,512]{1,0:T(8,128)S(1)} %copy.51), channel_id=1, source_target_pairs={{0,4},{4,8},{8,12},{12,16},{16,20},{20,24},{24,28},{28,0},{1,5},{5... | collective-permute-start | bytes 67592 | tf_op jit(solution)/shard_map/ppermute | solution.py:12
  71.1 5.3 %collective-permute-start.1 = (f32[7,512]{1,0:T(8,128)S(1)}, f32[7,512]{1,0:T(8,128)S(1)}, u32[]{:S(2)}, u32[]{:S(2)}) collective-permute-start(f32[7,512]{1,0:T(8,128)S(1)} %all_gather.3), channel_id=1, source_target_pairs={{0,28},{4,0},{8,4},{12,8},{16,12},{20,16},{24,20},{28,24},{1,29},{... | collective-permute-start | bytes 43016 | tf_op jit(solution)/shard_map/ppermute | solution.py:12
Sparse Core Ops, SparseCore 0:
  24.3 18.2 reduce-scatter.1
where the time goes:
time: 86.3 us; the launch traced here: 85.7 us
  blocking collectives  44 us (51%)
  between operations  14.8 us (17%)
  other arithmetic  10.3 us (12%)
  starting transfers between devices  6.41 us (7%)
  local copies, waits for them, and re-layouts  5.38 us (6%)
  waiting for transfers between devices  4.84 us (6%)
    psum x1, blocking collectives, local(): total = lax.psum(jnp.sum(moments[0]), ('grp', 'dom'))  38.2 us
    ppermute x2, starting transfers between devices, from_behind(): lax.ppermute(shard, axis, [(i, (i + by) % devices) for i in range(devices)])  6.37 us
    all_gather x1, blocking collectives, local(): group_stats = lax.all_gather(halo_table[1:8], 'dom', axis=1, tiled=True)  5.74 us
    ppermute x2, waiting for transfers between devices, from_behind(): lax.ppermute(shard, axis, [(i, (i + by) % devices) for i in range(devices)])  4.82 us
    unnamed x14, local copies, waits for them, and re-layouts  1.75 us
  transfers between devices with their start and end apart: 3, of which 1 were waited for; matrix products, arithmetic and copies ran while one was open for 2% of the time, Pallas kernels for 0%

commit v1 on v0

v1 whole, which is shorter than its diff:
```python
import functools

import jax
import jax.numpy as jnp
from jax import lax
from jax.experimental import pallas as pl
from jax.experimental.pallas import tpu as pltpu
from jax.sharding import PartitionSpec as P

BOX = 1.0
EPSILON = 1e-06
MESH = pl.DeviceIdType.MESH
F32 = jnp.float32
BF16 = jnp.bfloat16
LANES = 128
CHUNKS = 4
MASS_ROW = 11


def pieces(x):
    hi = x.astype(BF16).astype(F32)
    rest = x - hi
    mid = rest.astype(BF16).astype(F32)
    return hi, mid, rest - mid


def quotient(x, n):
    return x >> (n.bit_length() - 1) if n & (n - 1) == 0 else x // n


def crossed(a, b):
    return (a[1] * b[2] - a[2] * b[1], a[2] * b[0] - a[0] * b[2], a[0] * b[1] - a[1] * b[0])


def kernel(
    groups, domains, owned, halos,
    pos_hbm, vel_hbm, mass_hbm, halo_ref, shift_ref, live_ref, count_ref, home_ref,
    table_ref, kin_hbm, rad_hbm,
    pos, vel, mass, kin, rad, cols, moments, tables, sums_in, stats, total_out, totals_in,
    in_sem, out_sem, send1, recv1, send2, recv2, send3, recv3,
):
    blocks, width = mass.shape
    rows = blocks // CHUNKS
    slots_n = 2 * domains
    g = lax.axis_index("grp")
    d = lax.axis_index("dom")

    def peer(dg, dd):
        return {"grp": lax.rem(g + dg % groups, groups), "dom": lax.rem(d + dd % domains, domains)}

    loads = []
    for c in range(CHUNKS):
        part = pl.ds(c * rows, rows)
        group = [
            pltpu.make_async_copy(mass_hbm.at[part], mass.at[part], in_sem.at[3 * c]),
            pltpu.make_async_copy(pos_hbm.at[:, part], pos.at[:, part], in_sem.at[3 * c + 1]),
            pltpu.make_async_copy(vel_hbm.at[:, part], vel.at[:, part], in_sem.at[3 * c + 2]),
        ]
        for copy in group:
            copy.start()
        loads.append(group)

    partners = {(0, dd) for dd in range(domains)}
    partners |= {(1 % groups, dd) for dd in range(domains)}
    partners |= {(-1 % groups, dd) for dd in range(domains)}
    partners |= {(dg, 0) for dg in range(groups)}
    partners = sorted(partners - {(0, 0)})
    barrier = pltpu.get_barrier_semaphore()
    for dg, dd in partners:
        pl.semaphore_signal(barrier, inc=1, device_id=peer(dg, dd), device_id_type=MESH)

    lane = lax.broadcasted_iota(jnp.int32, (blocks, LANES), 1)
    row = lax.broadcasted_iota(jnp.int32, (blocks, 1), 0)
    packed = jnp.concatenate(
        [
            halo_ref[...].astype(F32),
            live_ref[...].astype(F32),
            shift_ref[...].astype(F32) * BOX,
            jnp.zeros((LANES - 5, blocks), F32),
        ],
        axis=0,
    )
    turned = packed.T
    live_col = jnp.where(row < count_ref[0], turned[:, 1:2], 0.0)
    cols[...] = jnp.where(lane == 1, live_col, turned)

    halo = turned[:, 0:1].astype(jnp.int32)
    home = home_ref[...]
    home_rows = home.shape[0]
    row_pick = lax.broadcasted_iota(jnp.int32, (blocks, home_rows), 1) == quotient(halo, LANES)
    split = jnp.concatenate([(home >> 8).astype(F32), (home & 255).astype(F32)], axis=1)
    picked = jnp.dot(
        row_pick.astype(F32).astype(BF16), split.astype(BF16), preferred_element_type=F32
    )
    value = picked[:, :LANES] * 256.0 + picked[:, LANES:]
    slot = jnp.sum(jnp.where(lane == (halo & (LANES - 1)), value, 0.0), axis=1, keepdims=True)
    slot = slot.astype(jnp.int32)
    owner = quotient(slot, owned)
    owner_grp = quotient(owner, domains)
    turn = owner - owner_grp * domains - d
    turn = jnp.where(turn < 0, turn + domains, turn)
    column = (jnp.where(owner_grp == g, 0, domains) + turn) * owned + slot - owner * owned
    spread_lanes = lax.broadcasted_iota(jnp.int32, (blocks, slots_n * owned), 1)
    onehot = (spread_lanes == column).astype(F32).astype(BF16)

    lane8 = lax.broadcasted_iota(jnp.int32, (8, LANES), 1)
    position8 = lax.broadcasted_iota(jnp.int32, (8, width), 1).astype(F32)

    def fold(x):
        parts = [x[:, i * LANES:(i + 1) * LANES] for i in range(width // LANES)]
        return jnp.sum(functools.reduce(lambda a, b: a + b, parts), axis=1, keepdims=True)

    def moment_rows(start):
        at = pl.ds(start, 8)
        col = cols[at]
        w = jnp.where(position8 < col[:, 1:2], mass[at], 0.0)
        u = [pos[k, at] + col[:, 2 + k:3 + k] for k in range(3)]
        v = [vel[k, at] for k in range(3)]
        wv = [w * x for x in v]
        made = [w] + [w * x for x in u] + wv
        made += [wv[0] * v[0] + wv[1] * v[1] + wv[2] * v[2]]
        made += list(crossed(u, wv))
        out = jnp.zeros((8, LANES), F32)
        for k, x in enumerate(made):
            out = jnp.where(lane8 == k, fold(x), out)
        moments[at] = out

    for c in range(CHUNKS):
        for copy in loads[c]:
            copy.wait()

        def step(i, carry, c=c):
            moment_rows(pl.multiple_of(c * rows + i * 8, 8))
            return carry

        lax.fori_loop(0, rows // 8, step, 0, unroll=True)

    by_row = moments[...].T[:16]
    mass_sum = jnp.sum(by_row[0:1], axis=1, keepdims=True)
    stacked = jnp.concatenate(pieces(by_row), axis=0).astype(BF16)
    product = jnp.dot(stacked, onehot, preferred_element_type=F32)
    product = product[:16] + product[16:32] + product[32:48]
    row16 = lax.broadcasted_iota(jnp.int32, (16, owned), 0)
    for k in range(slots_n):
        tables[k] = jnp.where(row16 == MASS_ROW, mass_sum, product[:, k * owned:(k + 1) * owned])

    pl.semaphore_wait(barrier, len(partners))

    order = sorted(range(1, slots_n), key=lambda k: -k)
    first = {}
    for k in order:
        dg, dd = divmod(k, domains)
        first[k] = pltpu.make_async_remote_copy(
            src_ref=tables.at[k], dst_ref=sums_in.at[k],
            send_sem=send1.at[k], recv_sem=recv1.at[k],
            device_id=peer(dg, dd), device_id_type=MESH,
        )
        first[k].start()

    sums = tables[0]
    for k in range(1, domains):
        first[k].wait_recv()
        sums = sums + sums_in[k]
    group_total = sums[MASS_ROW:MASS_ROW + 1]
    total_out[0] = group_total
    for k in range(domains, slots_n):
        first[k].wait_recv()
        sums = sums + sums_in[k]

    heavy_inv = 1.0 / jnp.maximum(sums[0:1], 1.0)
    scaled = sums[1:11] * heavy_inv
    centre = [scaled[k:k + 1] for k in range(3)]
    drift = [scaled[3 + k:4 + k] for k in range(3)]
    spread = scaled[6:7] - (drift[0] * drift[0] + drift[1] * drift[1] + drift[2] * drift[2])
    stats[0] = jnp.concatenate(
        centre + drift + [spread, 1.0 / (3.0 * spread + EPSILON)], axis=0
    )
    turned_spin = crossed(centre, drift)
    spin = [scaled[7 + k:8 + k] - turned_spin[k] for k in range(3)]

    second = {}
    for k in order:
        dg, dd = divmod(k, domains)
        second[k] = pltpu.make_async_remote_copy(
            src_ref=stats.at[0], dst_ref=stats.at[k],
            send_sem=send2.at[k], recv_sem=recv2.at[k],
            device_id=peer(-dg, -dd), device_id_type=MESH,
        )
        second[k].start()
    third = {}
    for dg in range(1, groups):
        third[dg] = pltpu.make_async_remote_copy(
            src_ref=total_out.at[0], dst_ref=totals_in.at[dg],
            send_sem=send3.at[dg], recv_sem=recv3.at[dg],
            device_id=peer(dg, 0), device_id_type=MESH,
        )
        third[dg].start()

    for k in range(1, slots_n):
        second[k].wait_recv()
    every = jnp.concatenate([stats[k] for k in range(slots_n)], axis=1)
    gathered = jnp.zeros((blocks, 8), F32)
    for piece in pieces(every):
        gathered = gathered + lax.dot_general(
            onehot, piece.astype(BF16), (((1,), (1,)), ((), ())), preferred_element_type=F32
        )
    moments[:, 0:8] = gathered

    def output_rows(start):
        at = pl.ds(start, 8)
        col = cols[at]
        mean = moments[at]
        live = position8 < col[:, 1:2]
        kinetic = 0.0
        radial = 0.0
        for k in range(3):
            distance = (pos[k, at] + col[:, 2 + k:3 + k]) - mean[:, k:k + 1]
            radial = radial + distance * distance
            offset = vel[k, at] - mean[:, 3 + k:4 + k]
            kinetic = kinetic + offset * offset
        kin[at] = jnp.where(live, kinetic * mean[:, 7:8], 0.0)
        rad[at] = jnp.where(live, radial, 0.0)

    stores = []
    for c in range(CHUNKS):

        def step(i, carry, c=c):
            output_rows(pl.multiple_of(c * rows + i * 8, 8))
            return carry

        lax.fori_loop(0, rows // 8, step, 0, unroll=True)
        part = pl.ds(c * rows, rows)
        group = [
            pltpu.make_async_copy(kin.at[part], kin_hbm.at[part], out_sem.at[2 * c]),
            pltpu.make_async_copy(rad.at[part], rad_hbm.at[part], out_sem.at[2 * c + 1]),
        ]
        for copy in group:
            copy.start()
        stores += group

    total = group_total
    for dg in range(1, groups):
        third[dg].wait_recv()
        total = total + totals_in[dg]
    share = sums[0:1] * float(halos) / total
    table_ref[...] = jnp.concatenate([share] + centre + drift + [spread] + spin, axis=0)

    for k in order:
        first[k].wait_send()
        second[k].wait_send()
    for dg in range(1, groups):
        third[dg].wait_send()
    for copy in stores:
        copy.wait()


def solution(mesh):
    groups, domains = mesh.shape["grp"], mesh.shape["dom"]

    def local(
        positions, velocities, masses, block_halo, block_shift, block_live, block_count, home_slot
    ):
        blocks, width = masses.shape
        halos = home_slot.shape[0]
        owned = halos // (groups * domains)
        slots_n = 2 * domains
        vmem = pl.BlockSpec(memory_space=pltpu.VMEM)
        smem = pl.BlockSpec(memory_space=pltpu.SMEM)
        hbm = pl.BlockSpec(memory_space=pl.ANY)
        dma = pltpu.SemaphoreType.DMA
        return pl.pallas_call(
            functools.partial(kernel, groups, domains, owned, halos),
            out_shape=(
                jax.ShapeDtypeStruct((11, owned), F32),
                jax.ShapeDtypeStruct((blocks, width), F32),
                jax.ShapeDtypeStruct((blocks, width), F32),
            ),
            in_specs=[hbm, hbm, hbm, vmem, vmem, vmem, smem, vmem],
            out_specs=(vmem, hbm, hbm),
            scratch_shapes=[
                pltpu.VMEM((3, blocks, width), F32),
                pltpu.VMEM((3, blocks, width), F32),
                pltpu.VMEM((blocks, width), F32),
                pltpu.VMEM((blocks, width), F32),
                pltpu.VMEM((blocks, width), F32),
                pltpu.VMEM((blocks, LANES), F32),
                pltpu.VMEM((blocks, LANES), F32),
                pltpu.VMEM((slots_n, 16, owned), F32),
                pltpu.VMEM((slots_n, 16, owned), F32),
                pltpu.VMEM((slots_n, 8, owned), F32),
                pltpu.VMEM((1, 1, owned), F32),
                pltpu.VMEM((groups, 1, owned), F32),
                dma((3 * CHUNKS,)),
                dma((2 * CHUNKS,)),
                dma((slots_n,)),
                dma((slots_n,)),
                dma((slots_n,)),
                dma((slots_n,)),
                dma((groups,)),
                dma((groups,)),
            ],
            compiler_params=pltpu.CompilerParams(collective_id=0, has_side_effects=True),
        )(
            positions, velocities, masses,
            block_halo.reshape(1, blocks), block_shift, block_live.reshape(1, blocks),
            block_count, home_slot.reshape(halos // LANES, LANES),
        )

    return jax.shard_map(
        local,
        mesh=mesh,
        in_specs=(
            P(None, ("grp", "dom"), None),
            P(None, ("grp", "dom"), None),
            P(("grp", "dom"), None),
            P(("grp", "dom")),
            P(None, ("grp", "dom")),
            P(("grp", "dom")),
            P(("grp", "dom")),
            P(),
        ),
        out_specs=(P(None, ("grp", "dom")), P(("grp", "dom"), None), P(("grp", "dom"), None)),
        check_vma=False,
    )
```

time: 86.3 us -> 22 us (0.25)
  blocking collectives: 44 us -> 0 us
  Pallas kernels: 0 us -> 16.7 us
  between operations: 14.8 us -> 1.29 us
  other arithmetic: 10.3 us -> 0 us
  starting transfers between devices: 6.41 us -> 0 us
  waiting for transfers between devices: 4.84 us -> 0 us
  local copies, waits for them, and re-layouts: 5.38 us -> 3.72 us
    psum x1 -> x0, blocking collectives: 38.2 us -> none  [local(): total = lax.psum(jnp.sum(moments[0]), ('grp', 'dom'))]
    pallas_call x0 -> x1, Pallas kernels: none -> 16.7 us  [local(): pl.pallas_call(functools.partial(kernel, groups, domains, owned, halos),...]
    ppermute x2 -> x0, starting transfers between devices: 6.37 us -> none  [from_behind(): lax.ppermute(shard, axis, [(i, (i + by) % devices) for i in range(devices)])]
    all_gather x1 -> x0, blocking collectives: 5.74 us -> none  [local(): group_stats = lax.all_gather(halo_table[1:8], 'dom', axis=1, tiled=True)]
    ppermute x2 -> x0, waiting for transfers between devices: 4.82 us -> none  [from_behind(): lax.ppermute(shard, axis, [(i, (i + by) % devices) for i in range(devices)])]
    sub x4 -> x0, other arithmetic: 2.27 us -> none  [the longest x1 1.41 us: halo_properties(): spread = sums[7] / heavy - jnp.sum(drift * drift, axis=0)]
    reduce_sum x4 -> x0, other arithmetic: 2.24 us -> none  [the longest x1 0.79 us: local(): total = lax.psum(jnp.sum(moments[0]), ('grp', 'dom'))]
    add x3 -> x0, other arithmetic: 2.12 us -> none  [the longest x1 1.32 us: block_moments(): positions + BOX * block_shift.astype(positions.dtype)[:, :, None]]
  transfers between devices with their start and end apart: 3 -> 0, of which waited for: 1 -> 0; matrix products, arithmetic and copies ran while one was open for 2% -> 0% of each run, Pallas kernels for 0% -> 0%
where the time goes in v1:
time: 22 us; the launch traced here: 21.7 us
  Pallas kernels  16.7 us (76%)
  local copies, waits for them, and re-layouts  3.72 us (17%)
  between operations  1.29 us (6%)
    pallas_call x1, Pallas kernels, local(): pl.pallas_call(functools.partial(kernel, groups, domains, owned, halos),...  16.7 us
    unnamed x5, local copies, waits for them, and re-layouts  3.72 us

profile of v1, /device:TPU:0, one launch (start us, length us, event | category | flops | bytes accessed | tf_op | source)
XLA Modules:
  0.0 21.7 jit_solution(13558282653507036081)
XLA Ops:
  1.3 16.7 %shard_map.103 = (f32[11,128]{1,0:T(8,128)}, f32[128,512]{1,0:T(8,128)}, f32[128,512]{1,0:T(8,128)}) custom-call(f32[3,128,512]{2,1,0:T(8,128)} %pos_hbm.1, f32[3,128,512]{2,1,0:T(8,128)} %vel_hbm.1, f32[128,512]{1,0:T(8,128)} %mass_hbm.1, s32[1,128]{1,0:T(1,128)} %bitcast.4, s32[3,128]{1,0:T(4,128)} %shift_ref.1, s32[1,128]{1,0:T(1,128)} %bitcast.5, ...), custom_call_target="tpu_custom_call" | custom-call | tf_op jit(solution)/shard_map/pallas_call | solution.py:271
  18.0 1.3 %copy.15 = f32[11,128]{1,0:T(8,128)} copy(f32[11,128]{1,0:T(8,128)} %get-tuple-element.6) | data formatting | bytes 11264
  19.3 0.0 copy-start
  19.3 1.7 %copy.16 = f32[128,512]{1,0:T(8,128)} copy(f32[128,512]{1,0:T(8,128)} %get-tuple-element.7) | data formatting | bytes 524288
  21.0 0.0 copy-done
  21.0 0.7 %copy.17 = f32[128,512]{1,0:T(8,128)} copy(f32[128,512]{1,0:T(8,128)S(1)} %copy-done) | data formatting | bytes 524288
Async XLA Ops:
  19.3 1.7 %copy-start = (f32[128,512]{1,0:T(8,128)S(1)}, f32[128,512]{1,0:T(8,128)}, u32[]{:S(2)}) copy-start(f32[128,512]{1,0:T(8,128)} %get-tuple-element.8) | copy-start | bytes 786436

commit v2 on v1

v2 whole, which is shorter than its diff:
```python
import functools

import jax
import jax.numpy as jnp
from jax import lax
from jax.experimental import pallas as pl
from jax.experimental.pallas import tpu as pltpu
from jax.sharding import PartitionSpec as P

BOX = 1.0
EPSILON = 1e-06
MESH = pl.DeviceIdType.MESH
F32 = jnp.float32
BF16 = jnp.bfloat16
LANES = 128
CHUNKS = 4
MASS_ROW = 11


def pieces(x):
    hi = x.astype(BF16).astype(F32)
    rest = x - hi
    mid = rest.astype(BF16).astype(F32)
    return hi, mid, rest - mid


def quotient(x, n):
    return x >> (n.bit_length() - 1) if n & (n - 1) == 0 else x // n


def crossed(a, b):
    return (a[1] * b[2] - a[2] * b[1], a[2] * b[0] - a[0] * b[2], a[0] * b[1] - a[1] * b[0])


def exchange_kernel(
    groups, domains, owned,
    pos_hbm, vel_hbm, mass_hbm, halo_ref, shift_ref, live_ref, count_ref, home_ref,
    pos, vel, means_ref, sums_ref,
    mass, cols, moments, tables, parts_in, own, near_in, ahead_in, behind_in, rest_in, totals_in,
    in_sem, send1, recv1, send_near, recv_near, send_up, recv_up, send_down, recv_down,
    send_rest, recv_rest, send_total, recv_total,
):
    blocks, width = mass.shape
    rows = blocks // CHUNKS
    g = lax.axis_index("grp")
    d = lax.axis_index("dom")

    def peer(dg, dd):
        return {"grp": lax.rem(g + dg % groups, groups), "dom": lax.rem(d + dd % domains, domains)}

    def remote(src, dst, send, recv, dg, dd):
        return pltpu.make_async_remote_copy(
            src_ref=src, dst_ref=dst, send_sem=send, recv_sem=recv,
            device_id=peer(dg, dd), device_id_type=MESH,
        )

    partners = {(0, dd) for dd in range(domains)}
    partners |= {(1 % groups, dd) for dd in range(domains)}
    partners |= {(-1 % groups, dd) for dd in range(domains)}
    partners |= {(dg, 0) for dg in range(groups)}
    partners = sorted(partners - {(0, 0)})
    barrier = pltpu.get_barrier_semaphore()
    for dg, dd in partners:
        pl.semaphore_signal(barrier, inc=1, device_id=peer(dg, dd), device_id_type=MESH)

    loads = []
    for c in range(CHUNKS):
        part = pl.ds(c * rows, rows)
        group = [
            pltpu.make_async_copy(mass_hbm.at[part], mass.at[part], in_sem.at[3 * c]),
            pltpu.make_async_copy(pos_hbm.at[:, part], pos.at[:, part], in_sem.at[3 * c + 1]),
            pltpu.make_async_copy(vel_hbm.at[:, part], vel.at[:, part], in_sem.at[3 * c + 2]),
        ]
        for copy in group:
            copy.start()
        loads.append(group)

    lane = lax.broadcasted_iota(jnp.int32, (blocks, LANES), 1)
    row = lax.broadcasted_iota(jnp.int32, (blocks, 1), 0)
    packed = jnp.concatenate(
        [
            halo_ref[...].astype(F32),
            live_ref[...].astype(F32),
            shift_ref[...].astype(F32) * BOX,
            jnp.zeros((LANES - 5, blocks), F32),
        ],
        axis=0,
    )
    turned = packed.T
    live_col = jnp.where(row < count_ref[...], turned[:, 1:2], 0.0)
    cols[...] = jnp.where(lane == 1, live_col, turned)

    halo = turned[:, 0:1].astype(jnp.int32)
    home = home_ref[...]
    home_rows = home.shape[0]
    row_pick = lax.broadcasted_iota(jnp.int32, (blocks, home_rows), 1) == quotient(halo, LANES)
    split = jnp.concatenate([(home >> 8).astype(F32), (home & 255).astype(F32)], axis=1)
    picked = jnp.dot(
        row_pick.astype(F32).astype(BF16), split.astype(BF16), preferred_element_type=F32
    )
    value = picked[:, :LANES] * 256.0 + picked[:, LANES:]
    slot = jnp.sum(jnp.where(lane == (halo & (LANES - 1)), value, 0.0), axis=1, keepdims=True)
    slot = slot.astype(jnp.int32)
    owner = quotient(slot, owned)
    owner_grp = quotient(owner, domains)
    turn = owner - owner_grp * domains - d
    turn = jnp.where(turn < 0, turn + domains, turn)
    column = (jnp.where(owner_grp == g, 0, domains) + turn) * owned + slot - owner * owned
    spread_lanes = lax.broadcasted_iota(jnp.int32, (blocks, 2 * domains * owned), 1)
    onehot = (spread_lanes == column).astype(F32).astype(BF16)

    lane8 = lax.broadcasted_iota(jnp.int32, (8, LANES), 1)
    position8 = lax.broadcasted_iota(jnp.int32, (8, width), 1).astype(F32)

    def fold(x):
        parts = [x[:, i * LANES:(i + 1) * LANES] for i in range(width // LANES)]
        return jnp.sum(functools.reduce(lambda a, b: a + b, parts), axis=1, keepdims=True)

    def moment_rows(start):
        at = pl.ds(start, 8)
        col = cols[at]
        w = jnp.where(position8 < col[:, 1:2], mass[at], 0.0)
        u = [pos[k, at] + col[:, 2 + k:3 + k] for k in range(3)]
        v = [vel[k, at] for k in range(3)]
        wv = [w * x for x in v]
        made = [w] + [w * x for x in u] + wv
        made += [wv[0] * v[0] + wv[1] * v[1] + wv[2] * v[2]]
        made += list(crossed(u, wv))
        out = jnp.zeros((8, LANES), F32)
        for k, x in enumerate(made):
            out = jnp.where(lane8 == k, fold(x), out)
        moments[at] = out

    for c in range(CHUNKS):
        for copy in loads[c]:
            copy.wait()

        def step(i, carry, c=c):
            moment_rows(pl.multiple_of(c * rows + i * 8, 8))
            return carry

        lax.fori_loop(0, rows // 8, step, 0, unroll=True)

    by_row = moments[...].T[:16]
    mass_sum = jnp.sum(by_row[0:1], axis=1, keepdims=True)
    stacked = jnp.concatenate(pieces(by_row), axis=0).astype(BF16)
    product = jnp.dot(stacked, onehot, preferred_element_type=F32)
    product = product[:16] + product[16:32] + product[32:48]
    row8 = lax.broadcasted_iota(jnp.int32, (8, owned), 0)
    for dd in range(domains):
        for ahead in range(2):
            k = ahead * domains + dd
            tile = product[:, k * owned:(k + 1) * owned]
            tables[dd, ahead] = tile[:8]
            tables[dd, 2 + ahead] = jnp.where(row8 == MASS_ROW - 8, mass_sum, tile[8:])

    pl.semaphore_wait(barrier, len(partners))

    first = {}
    for dd in range(1, domains):
        first[dd] = remote(
            tables.at[dd], parts_in.at[dd], send1.at[dd], recv1.at[dd], 0, dd
        )
        first[dd].start()
    total_of = [tables[0, q] for q in range(4)]
    for dd in range(1, domains):
        first[dd].wait_recv()
        total_of = [total_of[q] + parts_in[dd, q] for q in range(4)]
    own[...] = jnp.stack(total_of, axis=0)
    mine, ahead = own.at[0], own.at[1]

    second = []
    for dd in list(range(1, domains)) + [0]:
        second.append(
            remote(ahead, behind_in.at[dd], send_up.at[dd], recv_up.at[dd], 1, -dd)
        )
        second.append(
            remote(mine, ahead_in.at[dd], send_down.at[dd], recv_down.at[dd], -1, -dd)
        )
    for dd in range(1, domains):
        second.append(
            remote(own.at[pl.ds(0, 2)], near_in.at[dd], send_near.at[dd], recv_near.at[dd], 0, -dd)
        )
    late = [remote(own.at[3], rest_in, send_rest, recv_rest, 1, 0)]
    for dg in range(1, groups):
        late.append(
            remote(
                own.at[2, pl.ds(MASS_ROW - 8, 1)], totals_in.at[dg],
                send_total.at[dg], recv_total.at[dg], dg, 0,
            )
        )
    for copy in second + late:
        copy.start()
    for copy in second:
        copy.wait_recv()

    here, there = [], []
    for dd in range(domains):
        near = [total_of[0], total_of[1]] if dd == 0 else [near_in[dd, 0], near_in[dd, 1]]
        here.append(near[0] + behind_in[dd])
        there.append(near[1] + ahead_in[dd])
    every = jnp.concatenate(here + there, axis=1)
    stacked = jnp.concatenate(list(pieces(every)) + [jnp.zeros_like(every)], axis=0).astype(BF16)
    gathered = lax.dot_general(
        stacked, onehot, (((1,), (1,)), ((), ())), preferred_element_type=F32
    )
    gathered = gathered[0:8] + gathered[8:16] + gathered[16:24]
    centre, drift, spread = halo_means(gathered)
    shifts = packed[2:5]
    live = jnp.where(
        lax.broadcasted_iota(jnp.int32, (1, blocks), 1) < count_ref[...], packed[1:2], 0.0
    )
    by_block = jnp.concatenate(
        [centre[k] - shifts[k:k + 1] for k in range(3)]
        + drift
        + [1.0 / (3.0 * spread + EPSILON), live, jnp.zeros((LANES - 8, blocks), F32)],
        axis=0,
    )
    means_ref[...] = by_block.T

    for copy in late:
        copy.wait_recv()
    total = total_of[2][MASS_ROW - 8:MASS_ROW - 7]
    for dg in range(1, groups):
        total = total + totals_in[dg]
    sums_ref[0:8] = here[0]
    sums_ref[8:16] = jnp.where(row8 == MASS_ROW - 8, total, total_of[2] + rest_in[...])

    for copy in list(first.values()) + second + late:
        copy.wait_send()


def halo_means(sums):
    scaled = sums[1:8] * (1.0 / jnp.maximum(sums[0:1], 1.0))
    centre = [scaled[k:k + 1] for k in range(3)]
    drift = [scaled[3 + k:4 + k] for k in range(3)]
    spread = scaled[6:7] - (drift[0] * drift[0] + drift[1] * drift[1] + drift[2] * drift[2])
    return centre, drift, spread


def output_kernel(
    halos, pos, vel, means_ref, sums_ref, table_hbm, kin_hbm, rad_hbm, table, kin, rad, sem
):
    blocks, width = kin.shape
    rows = blocks // CHUNKS
    position8 = lax.broadcasted_iota(jnp.int32, (8, width), 1).astype(F32)

    sums = sums_ref[...]
    centre, drift, spread = halo_means(sums)
    heavy_inv = 1.0 / jnp.maximum(sums[0:1], 1.0)
    turned_spin = crossed(centre, drift)
    spin = [sums[8 + k:9 + k] * heavy_inv - turned_spin[k] for k in range(3)]
    share = sums[0:1] * float(halos) / sums[MASS_ROW:MASS_ROW + 1]
    table[...] = jnp.concatenate([share] + centre + drift + [spread] + spin, axis=0)
    stores = [pltpu.make_async_copy(table, table_hbm, sem.at[2 * CHUNKS])]
    stores[0].start()

    def output_rows(start):
        at = pl.ds(start, 8)
        mean = means_ref[at]
        live = position8 < mean[:, 7:8]
        kinetic = 0.0
        radial = 0.0
        for k in range(3):
            distance = pos[k, at] - mean[:, k:k + 1]
            radial = radial + distance * distance
            offset = vel[k, at] - mean[:, 3 + k:4 + k]
            kinetic = kinetic + offset * offset
        kin[at] = jnp.where(live, kinetic * mean[:, 6:7], 0.0)
        rad[at] = jnp.where(live, radial, 0.0)

    for c in range(CHUNKS):

        def step(i, carry, c=c):
            output_rows(pl.multiple_of(c * rows + i * 8, 8))
            return carry

        lax.fori_loop(0, rows // 8, step, 0, unroll=True)
        part = pl.ds(c * rows, rows)
        group = [
            pltpu.make_async_copy(kin.at[part], kin_hbm.at[part], sem.at[2 * c]),
            pltpu.make_async_copy(rad.at[part], rad_hbm.at[part], sem.at[2 * c + 1]),
        ]
        for copy in group:
            copy.start()
        stores += group
    for copy in stores:
        copy.wait()


def solution(mesh):
    groups, domains = mesh.shape["grp"], mesh.shape["dom"]

    def local(
        positions, velocities, masses, block_halo, block_shift, block_live, block_count, home_slot
    ):
        blocks, width = masses.shape
        halos = home_slot.shape[0]
        owned = halos // (groups * domains)
        vmem = pl.BlockSpec(memory_space=pltpu.VMEM)
        hbm = pl.BlockSpec(memory_space=pl.ANY)
        dma = pltpu.SemaphoreType.DMA
        pos, vel, means, sums = pl.pallas_call(
            functools.partial(exchange_kernel, groups, domains, owned),
            out_shape=(
                pltpu.VMEM((3, blocks, width), F32),
                pltpu.VMEM((3, blocks, width), F32),
                pltpu.VMEM((blocks, LANES), F32),
                pltpu.VMEM((16, owned), F32),
            ),
            in_specs=[hbm, hbm, hbm, vmem, vmem, vmem, vmem, vmem],
            out_specs=(vmem, vmem, vmem, vmem),
            scratch_shapes=[
                pltpu.VMEM((blocks, width), F32),
                pltpu.VMEM((blocks, LANES), F32),
                pltpu.VMEM((blocks, LANES), F32),
                pltpu.VMEM((domains, 4, 8, owned), F32),
                pltpu.VMEM((domains, 4, 8, owned), F32),
                pltpu.VMEM((4, 8, owned), F32),
                pltpu.VMEM((domains, 2, 8, owned), F32),
                pltpu.VMEM((domains, 8, owned), F32),
                pltpu.VMEM((domains, 8, owned), F32),
                pltpu.VMEM((8, owned), F32),
                pltpu.VMEM((groups, 1, owned), F32),
                dma((3 * CHUNKS,)),
                dma((domains,)), dma((domains,)),
                dma((domains,)), dma((domains,)),
                dma((domains,)), dma((domains,)),
                dma((domains,)), dma((domains,)),
                dma, dma,
                dma((groups,)), dma((groups,)),
            ],
            compiler_params=pltpu.CompilerParams(collective_id=0, has_side_effects=True),
        )(
            positions, velocities, masses,
            block_halo.reshape(1, blocks), block_shift, block_live.reshape(1, blocks),
            block_count.reshape(1, 1), home_slot.reshape(halos // LANES, LANES),
        )
        return pl.pallas_call(
            functools.partial(output_kernel, halos),
            out_shape=(
                jax.ShapeDtypeStruct((11, owned), F32),
                jax.ShapeDtypeStruct((blocks, width), F32),
                jax.ShapeDtypeStruct((blocks, width), F32),
            ),
            in_specs=[vmem, vmem, vmem, vmem],
            out_specs=(hbm, hbm, hbm),
            scratch_shapes=[
                pltpu.VMEM((11, owned), F32),
                pltpu.VMEM((blocks, width), F32),
                pltpu.VMEM((blocks, width), F32),
                dma((2 * CHUNKS + 1,)),
            ],
        )(*[pltpu.with_memory_space_constraint(x, pltpu.VMEM) for x in (pos, vel, means, sums)])

    return jax.shard_map(
        local,
        mesh=mesh,
        in_specs=(
            P(None, ("grp", "dom"), None),
            P(None, ("grp", "dom"), None),
            P(("grp", "dom"), None),
            P(("grp", "dom")),
            P(None, ("grp", "dom")),
            P(("grp", "dom")),
            P(("grp", "dom")),
            P(),
        ),
        out_specs=(P(None, ("grp", "dom")), P(("grp", "dom"), None), P(("grp", "dom"), None)),
        check_vma=False,
    )
```

time: 22 us -> 17.8 us (0.81)
  local copies, waits for them, and re-layouts: 3.72 us -> 0 us
  Pallas kernels: 16.7 us -> 16.2 us
    unnamed x5 -> x0, local copies, waits for them, and re-layouts: 3.72 us -> none
    pallas_call x1 -> x2, Pallas kernels: 16.7 us -> 16.2 us  [the longest x1 15.2 us: local(): pl.pallas_call(functools.partial(exchange_kernel, groups, domains, owned)...]
where the time goes in v2:
time: 17.8 us; the launch traced here: 17.5 us
  Pallas kernels  16.2 us (91%)
  between operations  1.29 us (7%)
    pallas_call x1, Pallas kernels, local(): pl.pallas_call(functools.partial(exchange_kernel, groups, domains, owned)...  15.2 us
    pallas_call x1, Pallas kernels, local(): pl.pallas_call(functools.partial(output_kernel, halos), out_shape=(jax.Sh...  1.04 us

profile of v2, /device:TPU:0, one launch (start us, length us, event | category | flops | bytes accessed | tf_op | source)
XLA Modules:
  0.0 17.5 jit_solution(15171269862170149970)
XLA Ops:
  1.3 15.2 %shard_map.103 = (f32[3,128,512]{2,1,0:T(8,128)S(1)}, f32[3,128,512]{2,1,0:T(8,128)S(1)}, f32[128,128]{1,0:T(8,128)S(1)}, f32[16,128]{1,0:T(8,128)S(1)}) custom-call(f32[3,128,512]{2,1,0:T(8,128)} %pos_hbm.1, f32[3,128,512]{2,1,0:T(8,128)} %vel_hbm.1, f32[128,512]{1,0:T(8,128)} %mass_hbm.1, s32[1,128]{1,0:T(1,128)} %bitcast.6, s32[3,128]{1,0:T(4,128)} %shift_ref.1, ...), custom_call_target="tpu_custom_call" | custom-call | tf_op jit(solution)/shard_map/pallas_call | solution.py:303
  16.5 1.0 %shard_map.104 = (f32[11,128]{1,0:T(8,128)}, f32[128,512]{1,0:T(8,128)}, f32[128,512]{1,0:T(8,128)}) custom-call(f32[3,128,512]{2,1,0:T(8,128)S(1)} %get-tuple-element.7.pos, f32[3,128,512]{2,1,0:T(8,128)S(1)} %get-tuple-element.8.vel, f32[128,128]{1,0:T(8,128)S(1)} %get-tuple-element.9.means_ref, f32[16,128]{1,0:T(8,128)S(1)} %get-tuple-element.10.sums_ref), custom_call_target="tpu_custom_call" | custom-call | tf_op jit(solution)/shard_map/pallas_call | solution.py:339

commit v3 on v2

--- a/solution.py
+++ b/solution.py
@@ -34,10 +34,10 @@
 
 def exchange_kernel(
     groups, domains, owned,
-    pos_hbm, vel_hbm, mass_hbm, halo_ref, shift_ref, live_ref, count_ref, home_ref,
+    pos_hbm, vel_hbm, mass_hbm, halo_hbm, shift_hbm, live_hbm, count_ref, home_hbm,
     pos, vel, means_ref, sums_ref,
-    mass, cols, moments, tables, parts_in, own, near_in, ahead_in, behind_in, rest_in, totals_in,
-    in_sem, send1, recv1, send_near, recv_near, send_up, recv_up, send_down, recv_down,
+    halo_ref, shift_ref, live_ref, home_ref, small_sem, mass, cols, moments, tables, parts_in, own, own_rest, near_in, ahead_in, behind_in, rest_in, totals_in,
+    in_sem, send1, recv1, send1b, recv1b, send_near, recv_near, send_up, recv_up, send_down, recv_down,
     send_rest, recv_rest, send_total, recv_total,
 ):
     blocks, width = mass.shape
@@ -54,15 +54,12 @@
             device_id=peer(dg, dd), device_id_type=MESH,
         )
 
-    partners = {(0, dd) for dd in range(domains)}
-    partners |= {(1 % groups, dd) for dd in range(domains)}
-    partners |= {(-1 % groups, dd) for dd in range(domains)}
-    partners |= {(dg, 0) for dg in range(groups)}
-    partners = sorted(partners - {(0, 0)})
-    barrier = pltpu.get_barrier_semaphore()
-    for dg, dd in partners:
-        pl.semaphore_signal(barrier, inc=1, device_id=peer(dg, dd), device_id_type=MESH)
-
+    pairs = ((halo_hbm, halo_ref), (live_hbm, live_ref), (shift_hbm, shift_ref), (home_hbm, home_ref))
+    smalls = [
+        pltpu.make_async_copy(src, dst, small_sem.at[k]) for k, (src, dst) in enumerate(pairs)
+    ]
+    for copy in smalls:
+        copy.start()
     loads = []
     for c in range(CHUNKS):
         part = pl.ds(c * rows, rows)
@@ -74,6 +71,18 @@
         for copy in group:
             copy.start()
         loads.append(group)
+
+    partners = {(0, dd) for dd in range(domains)}
+    partners |= {(1 % groups, dd) for dd in range(domains)}
+    partners |= {(-1 % groups, dd) for dd in range(domains)}
+    partners |= {(dg, 0) for dg in range(groups)}
+    partners = sorted(partners - {(0, 0)})
+    barrier = pltpu.get_barrier_semaphore()
+    for dg, dd in partners:
+        pl.semaphore_signal(barrier, inc=1, device_id=peer(dg, dd), device_id_type=MESH)
+
+    for copy in smalls:
+        copy.wait()
 
     lane = lax.broadcasted_iota(jnp.int32, (blocks, LANES), 1)
     row = lax.broadcasted_iota(jnp.int32, (blocks, 1), 0)
@@ -156,17 +165,20 @@
 
     pl.semaphore_wait(barrier, len(partners))
 
-    first = {}
-    for dd in range(1, domains):
-        first[dd] = remote(
-            tables.at[dd], parts_in.at[dd], send1.at[dd], recv1.at[dd], 0, dd
-        )
-        first[dd].start()
+    first, other = {}, {}
+    for part, copies, send, recv in ((0, first, send1, recv1), (2, other, send1b, recv1b)):
+        for dd in range(1, domains):
+            copies[dd] = remote(
+                tables.at[dd, pl.ds(part, 2)], parts_in.at[dd, pl.ds(part, 2)],
+                send.at[dd], recv.at[dd], 0, dd,
+            )
+            copies[dd].start()
     total_of = [tables[0, q] for q in range(4)]
     for dd in range(1, domains):
         first[dd].wait_recv()
-        total_of = [total_of[q] + parts_in[dd, q] for q in range(4)]
-    own[...] = jnp.stack(total_of, axis=0)
+        for q in range(2):
+            total_of[q] = total_of[q] + parts_in[dd, q]
+    own[...] = jnp.stack(total_of[:2], axis=0)
     mine, ahead = own.at[0], own.at[1]
 
     second = []
@@ -179,17 +191,25 @@
         )
     for dd in range(1, domains):
         second.append(
-            remote(own.at[pl.ds(0, 2)], near_in.at[dd], send_near.at[dd], recv_near.at[dd], 0, -dd)
-        )
-    late = [remote(own.at[3], rest_in, send_rest, recv_rest, 1, 0)]
+            remote(own, near_in.at[dd], send_near.at[dd], recv_near.at[dd], 0, -dd)
+        )
+    for copy in second:
+        copy.start()
+    for dd in range(1, domains):
+        other[dd].wait_recv()
+        for q in range(2, 4):
+            total_of[q] = total_of[q] + parts_in[dd, q]
+    own_rest[...] = jnp.stack(total_of[2:], axis=0)
+    late = []
     for dg in range(1, groups):
         late.append(
             remote(
-                own.at[2, pl.ds(MASS_ROW - 8, 1)], totals_in.at[dg],
+                own_rest.at[0, pl.ds(MASS_ROW - 8, 1)], totals_in.at[dg],
                 send_total.at[dg], recv_total.at[dg], dg, 0,
             )
         )
-    for copy in second + late:
+    late.append(remote(own_rest.at[1], rest_in, send_rest, recv_rest, 1, 0))
+    for copy in late:
         copy.start()
     for copy in second:
         copy.wait_recv()
@@ -226,7 +246,7 @@
     sums_ref[0:8] = here[0]
     sums_ref[8:16] = jnp.where(row8 == MASS_ROW - 8, total, total_of[2] + rest_in[...])
 
-    for copy in list(first.values()) + second + late:
+    for copy in list(first.values()) + list(other.values()) + second + late:
         copy.wait_send()
 
 
@@ -308,21 +328,28 @@
                 pltpu.VMEM((blocks, LANES), F32),
                 pltpu.VMEM((16, owned), F32),
             ),
-            in_specs=[hbm, hbm, hbm, vmem, vmem, vmem, vmem, vmem],
+            in_specs=[hbm, hbm, hbm, hbm, hbm, hbm, vmem, hbm],
             out_specs=(vmem, vmem, vmem, vmem),
             scratch_shapes=[
+                pltpu.VMEM((1, blocks), jnp.int32),
+                pltpu.VMEM((3, blocks), jnp.int32),
+                pltpu.VMEM((1, blocks), jnp.int32),
+                pltpu.VMEM((halos // LANES, LANES), jnp.int32),
+                dma((4,)),
                 pltpu.VMEM((blocks, width), F32),
                 pltpu.VMEM((blocks, LANES), F32),
                 pltpu.VMEM((blocks, LANES), F32),
                 pltpu.VMEM((domains, 4, 8, owned), F32),
                 pltpu.VMEM((domains, 4, 8, owned), F32),
-                pltpu.VMEM((4, 8, owned), F32),
+                pltpu.VMEM((2, 8, owned), F32),
+                pltpu.VMEM((2, 8, owned), F32),
                 pltpu.VMEM((domains, 2, 8, owned), F32),
                 pltpu.VMEM((domains, 8, owned), F32),
                 pltpu.VMEM((domains, 8, owned), F32),
                 pltpu.VMEM((8, owned), F32),
                 pltpu.VMEM((groups, 1, owned), F32),
                 dma((3 * CHUNKS,)),
+                dma((domains,)), dma((domains,)),
                 dma((domains,)), dma((domains,)),
                 dma((domains,)), dma((domains,)),
                 dma((domains,)), dma((domains,)),

time: 17.8 us -> 17.6 us (0.989)
  no operation moved by 1% of the time
where the time goes in v3:
time: 17.6 us; the launch traced here: 17.4 us
  Pallas kernels  16.1 us (91%)
  between operations  1.29 us (7%)
    pallas_call x1, Pallas kernels, local(): pl.pallas_call(functools.partial(exchange_kernel, groups, domains, owned)...  15.1 us
    pallas_call x1, Pallas kernels, local(): pl.pallas_call(functools.partial(output_kernel, halos), out_shape=(jax.Sh...  1.04 us

profile of v3, /device:TPU:0, one launch (start us, length us, event | category | flops | bytes accessed | tf_op | source)
XLA Modules:
  0.0 17.4 jit_solution(12695760325231436333)
XLA Ops:
  1.3 15.1 %shard_map.103 = (f32[3,128,512]{2,1,0:T(8,128)S(1)}, f32[3,128,512]{2,1,0:T(8,128)S(1)}, f32[128,128]{1,0:T(8,128)S(1)}, f32[16,128]{1,0:T(8,128)S(1)}) custom-call(f32[3,128,512]{2,1,0:T(8,128)} %pos_hbm.1, f32[3,128,512]{2,1,0:T(8,128)} %vel_hbm.1, f32[128,512]{1,0:T(8,128)} %mass_hbm.1, s32[1,128]{1,0:T(1,128)} %bitcast.6, s32[3,128]{1,0:T(4,128)} %shift_hbm.1, ...), custom_call_target="tpu_custom_call" | custom-call | tf_op jit(solution)/shard_map/pallas_call | solution.py:323
  16.4 1.0 %shard_map.104 = (f32[11,128]{1,0:T(8,128)}, f32[128,512]{1,0:T(8,128)}, f32[128,512]{1,0:T(8,128)}) custom-call(f32[3,128,512]{2,1,0:T(8,128)S(1)} %get-tuple-element.7.pos, f32[3,128,512]{2,1,0:T(8,128)S(1)} %get-tuple-element.8.vel, f32[128,128]{1,0:T(8,128)S(1)} %get-tuple-element.9.means_ref, f32[16,128]{1,0:T(8,128)S(1)} %get-tuple-element.10.sums_ref), custom_call_target="tpu_custom_call" | custom-call | tf_op jit(solution)/shard_map/pallas_call | solution.py:366

commit v4 on v3

--- a/solution.py
+++ b/solution.py
@@ -13,7 +13,7 @@
 F32 = jnp.float32
 BF16 = jnp.bfloat16
 LANES = 128
-CHUNKS = 4
+CHUNKS = 2
 MASS_ROW = 11
 
 
@@ -36,7 +36,7 @@
     groups, domains, owned,
     pos_hbm, vel_hbm, mass_hbm, halo_hbm, shift_hbm, live_hbm, count_ref, home_hbm,
     pos, vel, means_ref, sums_ref,
-    halo_ref, shift_ref, live_ref, home_ref, small_sem, mass, cols, moments, tables, parts_in, own, own_rest, near_in, ahead_in, behind_in, rest_in, totals_in,
+    halo_ref, shift_ref, live_ref, home_ref, small_sem, mass, cols, moments, tables, parts_in, own, own_rest, total_out, near_in, ahead_in, behind_in, rest_in, totals_in,
     in_sem, send1, recv1, send1b, recv1b, send_near, recv_near, send_up, recv_up, send_down, recv_down,
     send_rest, recv_rest, send_total, recv_total,
 ):
@@ -68,8 +68,8 @@
             pltpu.make_async_copy(pos_hbm.at[:, part], pos.at[:, part], in_sem.at[3 * c + 1]),
             pltpu.make_async_copy(vel_hbm.at[:, part], vel.at[:, part], in_sem.at[3 * c + 2]),
         ]
-        for copy in group:
-            copy.start()
+        for n, copy in enumerate(group):
+            copy.start(priority=(c + n) % 2)
         loads.append(group)
 
     partners = {(0, dd) for dd in range(domains)}
@@ -166,19 +166,20 @@
     pl.semaphore_wait(barrier, len(partners))
 
     first, other = {}, {}
-    for part, copies, send, recv in ((0, first, send1, recv1), (2, other, send1b, recv1b)):
+    for part, size, copies, send, recv in ((0, 3, first, send1, recv1), (3, 1, other, send1b, recv1b)):
         for dd in range(1, domains):
             copies[dd] = remote(
-                tables.at[dd, pl.ds(part, 2)], parts_in.at[dd, pl.ds(part, 2)],
+                tables.at[dd, pl.ds(part, size)], parts_in.at[dd, pl.ds(part, size)],
                 send.at[dd], recv.at[dd], 0, dd,
             )
             copies[dd].start()
     total_of = [tables[0, q] for q in range(4)]
     for dd in range(1, domains):
         first[dd].wait_recv()
-        for q in range(2):
+        for q in range(3):
             total_of[q] = total_of[q] + parts_in[dd, q]
     own[...] = jnp.stack(total_of[:2], axis=0)
+    total_out[0] = total_of[2][MASS_ROW - 8:MASS_ROW - 7]
     mine, ahead = own.at[0], own.at[1]
 
     second = []
@@ -193,24 +194,22 @@
         second.append(
             remote(own, near_in.at[dd], send_near.at[dd], recv_near.at[dd], 0, -dd)
         )
-    for copy in second:
+    late = []
+    for dg in sorted(range(1, groups), key=lambda x: -min(x, groups - x)):
+        late.append(
+            remote(
+                total_out.at[0], totals_in.at[dg],
+                send_total.at[dg], recv_total.at[dg], dg, 0,
+            )
+        )
+    for copy in late + second:
         copy.start()
     for dd in range(1, domains):
         other[dd].wait_recv()
-        for q in range(2, 4):
-            total_of[q] = total_of[q] + parts_in[dd, q]
-    own_rest[...] = jnp.stack(total_of[2:], axis=0)
-    late = []
-    for dg in range(1, groups):
-        late.append(
-            remote(
-                own_rest.at[0, pl.ds(MASS_ROW - 8, 1)], totals_in.at[dg],
-                send_total.at[dg], recv_total.at[dg], dg, 0,
-            )
-        )
-    late.append(remote(own_rest.at[1], rest_in, send_rest, recv_rest, 1, 0))
-    for copy in late:
-        copy.start()
+        total_of[3] = total_of[3] + parts_in[dd, 3]
+    own_rest[...] = total_of[3]
+    late.append(remote(own_rest, rest_in, send_rest, recv_rest, 1, 0))
+    late[-1].start()
     for copy in second:
         copy.wait_recv()
 
@@ -342,7 +341,8 @@
                 pltpu.VMEM((domains, 4, 8, owned), F32),
                 pltpu.VMEM((domains, 4, 8, owned), F32),
                 pltpu.VMEM((2, 8, owned), F32),
-                pltpu.VMEM((2, 8, owned), F32),
+                pltpu.VMEM((8, owned), F32),
+                pltpu.VMEM((1, 1, owned), F32),
                 pltpu.VMEM((domains, 2, 8, owned), F32),
                 pltpu.VMEM((domains, 8, owned), F32),
                 pltpu.VMEM((domains, 8, owned), F32),

time: 17.6 us -> 17.2 us (0.977)
  Pallas kernels: 16.1 us -> 15.8 us
    pallas_call x1, Pallas kernels: 15.1 us -> 14.7 us  [local(): pl.pallas_call(functools.partial(exchange_kernel, groups, domains, owned)...]
where the time goes in v4:
time: 17.2 us; the launch traced here: 17 us
  Pallas kernels  15.8 us (92%)
  between operations  1.29 us (8%)
    pallas_call x1, Pallas kernels, local(): pl.pallas_call(functools.partial(exchange_kernel, groups, domains, owned)...  14.7 us
    pallas_call x1, Pallas kernels, local(): pl.pallas_call(functools.partial(output_kernel, halos), out_shape=(jax.Sh...  1.04 us

profile of v4, /device:TPU:0, one launch (start us, length us, event | category | flops | bytes accessed | tf_op | source)
XLA Modules:
  0.0 17.0 jit_solution(15024334753684994580)
XLA Ops:
  1.3 14.7 %shard_map.103 = (f32[3,128,512]{2,1,0:T(8,128)S(1)}, f32[3,128,512]{2,1,0:T(8,128)S(1)}, f32[128,128]{1,0:T(8,128)S(1)}, f32[16,128]{1,0:T(8,128)S(1)}) custom-call(f32[3,128,512]{2,1,0:T(8,128)} %pos_hbm.1, f32[3,128,512]{2,1,0:T(8,128)} %vel_hbm.1, f32[128,512]{1,0:T(8,128)} %mass_hbm.1, s32[1,128]{1,0:T(1,128)} %bitcast.6, s32[3,128]{1,0:T(4,128)} %shift_hbm.1, ...), custom_call_target="tpu_custom_call" | custom-call | tf_op jit(solution)/shard_map/pallas_call | solution.py:322
  16.0 1.0 %shard_map.104 = (f32[11,128]{1,0:T(8,128)}, f32[128,512]{1,0:T(8,128)}, f32[128,512]{1,0:T(8,128)}) custom-call(f32[3,128,512]{2,1,0:T(8,128)S(1)} %get-tuple-element.7.pos, f32[3,128,512]{2,1,0:T(8,128)S(1)} %get-tuple-element.8.vel, f32[128,128]{1,0:T(8,128)S(1)} %get-tuple-element.9.means_ref, f32[16,128]{1,0:T(8,128)S(1)} %get-tuple-element.10.sums_ref), custom_call_target="tpu_custom_call" | custom-call | tf_op jit(solution)/shard_map/pallas_call | solution.py:366
